TPU v7x, 32 devices: a whole 2x2x4 slice. The times are simulated.
32 devices in a mesh: samp: 16 (over z, y, core), snp: 2 (over x).
Axes of the slice: x: 2, y: 2, z: 4, core: 2. Of those that a mesh axis runs over, the one named last changes fastest.
Arguments:
- genotypes: float32 [8192, 2048], P('samp', 'snp'), may hold values from 0 to 2, as said below
- observed: int32 [8192, 2048], P('samp', 'snp'), may hold values from 0 to 1
Outputs:
- relation: float32 [16, 2, 256, 8192], P(None, 'snp', None, 'samp')
Inputs may be any that keep to these rules, and one draw needn't show every extreme that they name: `genotypes`: dosages are real numbers between 0 and 2.
All inputs are finite; a program needn't handle non-finite values.
Results may differ from a plain program's by a relative error of at most 0.00061.
Values may be sent and summed in bfloat16 or wider, within the bound.
A program may use at most 128 MiB of HBM per device.

v0:
```python
import jax
import jax.numpy as jnp
from jax import lax
from jax.sharding import PartitionSpec as P

var_floor = 0.1


def body(genotypes, observed):
    row_count, snp_count = genotypes.shape
    present = observed.astype(jnp.float32)
    alt_local = jnp.sum(present * genotypes, axis=0)
    call_local = jnp.sum(present, axis=0)
    alt_sum, call_sum = lax.psum((alt_local, call_local), "samp")
    frequency = alt_sum / (2.0 * jnp.maximum(call_sum, 1.0))
    variance = jnp.maximum(2.0 * frequency * (1.0 - frequency), var_floor)
    scaled = (present * (genotypes - 2.0 * frequency) * lax.rsqrt(variance)).astype(jnp.bfloat16)
    shards = lax.axis_size("samp")
    groups = lax.axis_size("snp")
    tile_rows = row_count // groups
    total_snps = snp_count * groups
    own_panel = lax.all_gather(scaled, "snp", axis=1, tiled=True)
    blocks = scaled.reshape(groups, tile_rows, snp_count)
    owned_rows = lax.all_to_all(blocks, "snp", split_axis=0, concat_axis=2, tiled=True)
    owned_rows = owned_rows.reshape(tile_rows, total_snps)
    summed = lax.dot_general(
        lax.all_gather(owned_rows, "samp", axis=0, tiled=True),
        own_panel,
        (((1,), (1,)), ((), ())),
        preferred_element_type=jnp.float32,
    )
    summed = summed.reshape(shards, 1, tile_rows, row_count)
    return summed / total_snps


def solution(mesh):
    return jax.shard_map(
        body,
        mesh=mesh,
        in_specs=(P("samp", "snp"), P("samp", "snp")),
        out_specs=P(None, "snp", None, "samp"),
        check_vma=False,
    )
```

profile of v0, /device:TPU:0, one launch (start us, length us, event | category | flops | bytes accessed | tf_op | source)
XLA Modules:
  0.0 236.2 jit_solution(17812353467611038530)
XLA Ops:
  6.5 0.0 copy-start
  6.5 0.0 all-gather.5.cloned.1.call-start
  6.5 2.8 %convert_reduce_fusion = (f32[1024]{0:T(1024)S(1)}, f32[1024]{0:T(1024)S(1)}) fusion(s32[512,1024]{1,0:T(8,128)} %param.3, f32[512,1024]{1,0:T(8,128)} %param.2), kind=kLoop, calls=%fused_computation.3 | loop fusion | flops 2095104 | bytes 4202496 | tf_op jit(solution)/shard_map/reduce_sum | solution.py:13
  9.4 35.5 %all-reduce = (f32[1024]{0:T(1024)S(1)}, f32[1024]{0:T(1024)S(1)}) all-reduce(f32[1024]{0:T(1024)S(1)} %get-tuple-element.6, f32[1024]{0:T(1024)S(1)} %get-tuple-element.5), channel_id=1, replica_groups=mesh['samp'=16,'snp'=2] {'samp'}, use_global_device_ids=true, to_apply=%region_1.0 | all-reduce | flops 2048 | bytes 16384 | tf_op jit(solution)/shard_map/psum | solution.py:14
  44.8 0.0 copy-done
  44.9 3.1 %multiply_convert_fusion = bf16[512,1024]{1,0:T(8,128)(2,1)} fusion(f32[512,1024]{1,0:T(8,128)S(1)} %copy-done, s32[512,1024]{1,0:T(8,128)} %param.3, f32[1024]{0:T(1024)S(1)} %get-tuple-element.10, f32[1024]{0:T(1024)S(1)} %get-tuple-element.9), kind=kLoop, calls=%fused_computation.1 | loop fusion | flops 2621440 | bytes 5251072 | tf_op jit(solution)/shard_map/convert_element_type | solution.py:17
  47.9 0.0 all-gather.5.cloned.1.call-update
  48.0 0.0 all-gather.3.cloned.1.call-start
  48.0 24.5 %all_to_all.15 = bf16[2,256,1024]{2,1,0:T(8,128)(2,1)S(1)} all-to-all(bf16[2,256,1024]{2,1,0:T(8,128)(2,1)} %bitcast.10), channel_id=1, replica_groups=mesh['samp'=16,'snp'=2] {'snp'}, dimensions={0} | all-to-all | bytes 2097152 | tf_op jit(solution)/shard_map/all_to_all | solution.py:24
  72.5 1.3 copy.5
  73.8 0.0 all-gather.3.cloned.1.call-update
  73.8 10.6 %all-gather.5.cloned.1.call-done = bf16[512,2048]{1,0:T(8,128)(2,1)} async-done(((bf16[512,1024]{1,0:T(8,128)(2,1)}), bf16[512,2048]{1,0:T(8,128)(2,1)}) %all-gather.5.cloned.1.call-update) | async-done | bytes 2097168 | tf_op jit(solution)/shard_map/all_gather | solution.py:22
  84.4 129.8 %all-gather.3.cloned.1.call-done = bf16[4096,2048]{0,1:T(8,128)(2,1)} async-done(((bf16[256,2048]{0,1:T(8,128)(2,1)}), bf16[4096,2048]{0,1:T(8,128)(2,1)}) %all-gather.3.cloned.1.call-update) | async-done | bytes 16777232 | tf_op jit(solution)/shard_map/all_gather | solution.py:27
  214.2 15.2 %convolution_multiply_fusion = f32[4096,512]{1,0:T(8,128)} fusion(bf16[4096,2048]{0,1:T(8,128)(2,1)} %all-gather.3.cloned.1.call-done, bf16[512,2048]{1,0:T(8,128)(2,1)} %all-gather.5.cloned.1.call-done), kind=kOutput, calls=%fused_computation | convolution fusion | flops 8592031744 | bytes 27262976 | tf_op jit(solution)/shard_map/dot_general | solution.py:26
  (1 shorter events, 0.0 us)
Async XLA Ops:
  6.5 38.3 %copy-start = (f32[512,1024]{1,0:T(8,128)S(1)}, f32[512,1024]{1,0:T(8,128)}, u32[]{:S(2)}) copy-start(f32[512,1024]{1,0:T(8,128)} %param.2) | copy-start | bytes 6291460
  6.5 77.9 %all-gather.5.cloned.1.call-start = ((), (), s32[]{:S(2)}) async-start(), calls=%async_computation.2 | async-start | bytes 3145728 | tf_op jit(solution)/shard_map/all_gather | solution.py:22
  48.0 166.2 %all-gather.3.cloned.1.call-start = ((), (), s32[]{:S(2)}) async-start(), calls=%async_computation.1 | async-start | bytes 17825792 | tf_op jit(solution)/shard_map/all_gather | solution.py:27
Sparse Core Ops, SparseCore 0:
  48.1 36.2 all-gather.4
  86.6 127.5 all-gather.2
where the time goes:
time: 236 us
  waiting for transfers between devices  140 us (59%)
  blocking collectives  60 us (25%)
  matrix products  15.2 us (6%)
  between operations  13.4 us (6%)
  other arithmetic  5.9 us (2%)
    all_gather x1, waiting for transfers between devices, body(): lax.all_gather(owned_rows, 'samp', axis=0, tiled=True)  130 us
    psum x1, blocking collectives, body(): alt_sum, call_sum = lax.psum((alt_local, call_local), 'samp')  35.5 us
    all_to_all x1, blocking collectives, body(): lax.all_to_all(blocks, 'snp', split_axis=0, concat_axis=2, tiled=True)  24.5 us
    dot_general x1, matrix products, body(): lax.dot_general(lax.all_gather(owned_rows, 'samp', axis=0, tiled=True), o...  15.2 us
    all_gather x1, waiting for transfers between devices, body(): own_panel = lax.all_gather(scaled, 'snp', axis=1, tiled=True)  10.6 us
  transfers between devices with their start and end apart: 2, of which 2 were waited for; matrix products, arithmetic and copies ran while one was open for 1% of the time, Pallas kernels for 0%

commit v1 on v0

v1 whole, which is shorter than its diff:
```python
import functools

import jax
import jax.numpy as jnp
from jax import lax
from jax.experimental import pallas as pl
from jax.experimental.pallas import tpu as pltpu
from jax.sharding import PartitionSpec as P

MESH = pl.DeviceIdType.MESH
var_floor = 0.1
UP, DOWN, SIDE, CORE = 0, 1, 2, 3
STRIP = 64


def kernel(shards, groups, geno_ref, obs_ref, out_ref, counts, panel, rows, tiles,
           count_send, count_recv, panel_send, panel_recv, row_send, row_recv, out_sem):
    row_count, snp_count = geno_ref.shape
    tile_rows = row_count // groups
    depth = shards // 4
    me = lax.axis_index("samp")
    part = lax.axis_index("snp")
    z, y, core = me // 4, (me // 2) % 2, me % 2

    def index(at_z, at_y, at_core):
        return at_z * 4 + at_y * 2 + at_core

    barrier = pltpu.get_barrier_semaphore()
    for step in range(1, shards):
        pl.semaphore_signal(barrier, inc=1, device_id={"samp": lax.rem(me + step, shards)}, device_id_type=MESH)
    for step in range(1, groups):
        pl.semaphore_signal(barrier, inc=1, device_id={"snp": lax.rem(part + step, groups)}, device_id_type=MESH)

    def add_strip(i, total):
        alt, call = total
        strip = pl.ds(pl.multiple_of(i * STRIP, STRIP), STRIP)
        present = obs_ref[strip, :].astype(jnp.float32)
        held = present * geno_ref[strip, :]
        for r in range(0, STRIP, 8):
            alt = alt + held[r:r + 8]
            call = call + present[r:r + 8]
        return alt, call

    zero = jnp.zeros((8, snp_count), jnp.float32)
    alt, call = lax.fori_loop(0, row_count // STRIP, add_strip, (zero, zero))
    counts[me, 0:1, :] = jnp.sum(alt, axis=0, keepdims=True)
    counts[me, 1:2, :] = jnp.sum(call, axis=0, keepdims=True)

    pl.semaphore_wait(barrier, shards + groups - 2)

    def count_copy(owner, to):
        return pltpu.make_async_remote_copy(
            src_ref=counts.at[owner], dst_ref=counts.at[owner], send_sem=count_send.at[to],
            recv_sem=count_recv.at[owner], device_id={"samp": to}, device_id_type=MESH)

    for step in range(1, shards):
        count_copy(me, lax.rem(me + step, shards)).start()
    for step in range(1, shards):
        other = lax.rem(me + step, shards)
        count_copy(other, other).wait_recv()
    sums = counts[0]
    for s in range(1, shards):
        sums = sums + counts[s]
    frequency = sums[0:1] / (2.0 * jnp.maximum(sums[1:2], 1.0))
    shift = 2.0 * frequency
    gain = lax.rsqrt(jnp.maximum(shift * (1.0 - frequency), var_floor))

    def panel_copy(h, k, to):
        block = panel.at[h, pl.ds(pl.multiple_of(k * tile_rows, tile_rows), tile_rows)]
        return pltpu.make_async_remote_copy(
            src_ref=block, dst_ref=block, send_sem=panel_send.at[to, k],
            recv_sem=panel_recv.at[h, k], device_id={"snp": to}, device_id_type=MESH)

    strip_rows = min(STRIP, tile_rows)

    def scale_tile(k):
        def scale_strip(i, carry):
            start = pl.multiple_of(k * tile_rows + i * strip_rows, strip_rows)
            strip = pl.ds(start, strip_rows)
            present = obs_ref[strip, :].astype(jnp.float32)
            panel[part, strip, :] = (present * (geno_ref[strip, :] - shift) * gain).astype(jnp.bfloat16)
            return carry

        lax.fori_loop(0, tile_rows // strip_rows, scale_strip, 0)

    def row_copy(q, h, way, src=None):
        to = (index(z + 1, y, core), index(z - 1, y, core), index(z, 1 - y, core), index(z, y, 1 - core))[way]
        return pltpu.make_async_remote_copy(
            src_ref=rows.at[q, h] if src is None else src, dst_ref=rows.at[q, h],
            send_sem=row_send.at[way, q, h], recv_sem=row_recv.at[q, h],
            device_id={"samp": to}, device_id_type=MESH)

    def arrive(q, h):
        row_copy(q, h, CORE).wait_recv()

    last_part = lax.rem(part + groups - 1, groups)
    turned = jnp.where(z < depth - 1, z + 1, depth - 2)

    def part_at(i):
        return lax.rem(part + i, groups)

    def source(i):
        pairs = jnp.minimum(z, depth - 1 - z)
        side = jnp.where(i % 2 == 1, z - (i + 1) // 2, z + i // 2)
        far = jnp.where(z < depth - 1 - z, z + i - pairs, z - i + pairs)
        return jnp.where(i <= 2 * pairs, side, far)

    def send_own(h):
        mine = panel.at[h, pl.ds(pl.multiple_of(part * tile_rows, tile_rows), tile_rows)]
        row_copy(me, h, SIDE, mine).start()

        @pl.when(z < depth - 1)
        def _():
            row_copy(me, h, UP, mine).start()

        @pl.when(z > 0)
        def _():
            row_copy(me, h, DOWN, mine).start()

        row_copy(me, h, CORE, mine).start()
        rows[me, h] = panel[h, pl.ds(pl.multiple_of(part * tile_rows, tile_rows), tile_rows), :]

    for step in range(1, groups):
        other = part_at(step)
        scale_tile(other)
        panel_copy(part, other, other).start()
    scale_tile(part)
    send_own(part)
    for step in range(1, groups):
        other = part_at(step)
        for k in range(1, groups):
            panel_copy(part, lax.rem(other + k, groups), other).start()
    for step in range(1, groups):
        h = part_at(step)
        panel_copy(h, part, h).wait_recv()
        send_own(h)

    def column_arrival(at_z, h, way):
        q = index(at_z, y, core)
        arrive(q, h)

        @pl.when(z < depth - 1 if way == UP else z > 0)
        def _():
            row_copy(q, h, way).start()

        @pl.when((at_z != turned) | (h != last_part))
        def _():
            row_copy(q, h, SIDE).start()

        row_copy(q, h, CORE).start()

    def column_arrivals(i):
        def per_part(t, carry):
            h = part_at(t)

            @pl.when(z - i >= 0)
            def _():
                column_arrival(z - i, h, UP)

            @pl.when(z + i < depth)
            def _():
                column_arrival(z + i, h, DOWN)

            return carry

        lax.fori_loop(0, groups, per_part, 0)

    def product(q):
        total = None
        for h in range(groups):
            term = lax.dot_general(rows[q, h], panel[h], (((1,), (1,)), ((), ())),
                                   preferred_element_type=jnp.float32)
            total = term if total is None else total + term
        tiles[q] = total * (1.0 / (groups * snp_count))
        pltpu.make_async_copy(tiles.at[q], out_ref.at[q, 0], out_sem.at[q]).start()

    def products(at_z, at_y):
        def per_core(t, carry):
            q = index(at_z, at_y, lax.rem(core + t, 2))

            @pl.when(t == 1)
            def _():
                for h in range(groups):
                    arrive(q, h)

            product(q)
            return carry

        lax.fori_loop(0, 2, per_core, 0)

    def side_arrival(at_z, h):
        q = index(at_z, 1 - y, core)
        arrive(q, h)
        row_copy(q, h, CORE).start()

    def round_of(i, carry):
        column_arrivals(i)

        @pl.when(i == 1)
        def _():
            for step in range(1, groups):
                h = part_at(step)
                for k in range(1, groups):
                    panel_copy(h, part_at(k), h).wait_recv()

        @pl.when(i == depth - 1)
        def _():
            q = index(z, 1 - y, core)

            @pl.when(z > 0)
            def _():
                row_copy(q, last_part, DOWN).start()

            @pl.when(z == depth - 2)
            def _():
                row_copy(q, last_part, UP).start()

        at_z = source(i - 1)
        products(at_z, y)

        def per_part(t, c):
            @pl.when((at_z != turned) | (t != groups - 1))
            def _():
                side_arrival(at_z, part_at(t))

            return c

        lax.fori_loop(0, groups, per_part, 0)

        @pl.when(at_z != turned)
        def _():
            products(at_z, 1 - y)

        return carry

    lax.fori_loop(1, depth + 1, round_of, 0)
    side_arrival(turned, last_part)
    products(turned, 1 - y)

    for step in range(1, shards):
        count_copy(me, lax.rem(me + step, shards)).wait_send()
    for step in range(1, groups):
        for k in range(groups):
            panel_copy(part, k, part_at(step)).wait_send()

    def drain(i, carry):
        at_z, h = i // groups, lax.rem(i, groups)
        q = index(at_z, y, core)
        across = index(at_z, 1 - y, core)

        @pl.when((at_z <= z) & (z < depth - 1))
        def _():
            row_copy(q, h, UP).wait_send()

        @pl.when((at_z >= z) & (z > 0))
        def _():
            row_copy(q, h, DOWN).wait_send()

        @pl.when((at_z != turned) | (h != last_part))
        def _():
            row_copy(q, h, SIDE).wait_send()

        row_copy(q, h, CORE).wait_send()
        row_copy(across, h, CORE).wait_send()

        @pl.when((at_z == z) & (h == last_part) & (z > 0))
        def _():
            row_copy(across, h, DOWN).wait_send()

        @pl.when((at_z == z) & (h == last_part) & (z == depth - 2))
        def _():
            row_copy(across, h, UP).wait_send()

        return carry

    lax.fori_loop(0, depth * groups, drain, 0)

    def flush(q, carry):
        pltpu.make_async_copy(tiles.at[q], out_ref.at[q, 0], out_sem.at[q]).wait()
        return carry

    lax.fori_loop(0, shards, flush, 0)


def solution(mesh):
    shards, groups = mesh.shape["samp"], mesh.shape["snp"]

    def body(genotypes, observed):
        row_count, snp_count = genotypes.shape
        tile_rows = row_count // groups
        return pl.pallas_call(
            functools.partial(kernel, shards, groups),
            out_shape=jax.ShapeDtypeStruct((shards, 1, tile_rows, row_count), jnp.float32),
            in_specs=[pl.BlockSpec(memory_space=pltpu.VMEM)] * 2,
            out_specs=pl.BlockSpec(memory_space=pl.ANY),
            scratch_shapes=[
                pltpu.VMEM((shards, 2, snp_count), jnp.float32),
                pltpu.VMEM((groups, row_count, snp_count), jnp.bfloat16),
                pltpu.VMEM((shards, groups, tile_rows, snp_count), jnp.bfloat16),
                pltpu.VMEM((shards, tile_rows, row_count), jnp.float32),
                pltpu.SemaphoreType.DMA((shards,)),
                pltpu.SemaphoreType.DMA((shards,)),
                pltpu.SemaphoreType.DMA((groups, groups)),
                pltpu.SemaphoreType.DMA((groups, groups)),
                pltpu.SemaphoreType.DMA((4, shards, groups)),
                pltpu.SemaphoreType.DMA((shards, groups)),
                pltpu.SemaphoreType.DMA((shards,)),
            ],
            compiler_params=pltpu.CompilerParams(
                collective_id=0, has_side_effects=True, vmem_limit_bytes=60 * 1024 * 1024),
        )(genotypes, observed)

    return jax.shard_map(
        body,
        mesh=mesh,
        in_specs=(P("samp", "snp"), P("samp", "snp")),
        out_specs=P(None, "snp", None, "samp"),
        check_vma=False,
    )
```

time: 236 us -> 111 us (0.47)
  waiting for transfers between devices: 140 us -> 0 us
  Pallas kernels: 0 us -> 103 us
  blocking collectives: 60 us -> 0 us
  matrix products: 15.2 us -> 0 us
  between operations: 13.4 us -> 0.01 us
  local copies, waits for them, and re-layouts: 1.32 us -> 8.12 us
  other arithmetic: 5.9 us -> 0 us
    all_gather x2 -> x0, waiting for transfers between devices: 140 us -> none  [the longest x1 130 us: body(): lax.all_gather(owned_rows, 'samp', axis=0, tiled=True)]
    pallas_call x0 -> x1, Pallas kernels: none -> 103 us  [body(): pl.pallas_call(functools.partial(kernel, shards, groups), out_shape=jax.S...]
    psum x1 -> x0, blocking collectives: 35.5 us -> none  [body(): alt_sum, call_sum = lax.psum((alt_local, call_local), 'samp')]
    all_to_all x1 -> x0, blocking collectives: 24.5 us -> none  [body(): lax.all_to_all(blocks, 'snp', split_axis=0, concat_axis=2, tiled=True)]
    dot_general x1 -> x0, matrix products: 15.2 us -> none  [body(): lax.dot_general(lax.all_gather(owned_rows, 'samp', axis=0, tiled=True), o...]
    unnamed x2 -> x1, local copies, waits for them, and re-layouts: 0.01 us -> 8.12 us
    convert_element_type x1 -> x0, other arithmetic: 3.08 us -> none  [body(): (present * (genotypes - 2.0 * frequency) * lax.rsqrt(variance)).astype(jn...]
    reduce_sum x1 -> x0, other arithmetic: 2.81 us -> none  [body(): call_local = jnp.sum(present, axis=0)]
  transfers between devices with their start and end apart: 2 -> 0, of which waited for: 2 -> 0; matrix products, arithmetic and copies ran while one was open for 1% -> 0% of each run, Pallas kernels for 0% -> 0%
where the time goes in v1:
time: 111 us
  Pallas kernels  103 us (93%)
  local copies, waits for them, and re-layouts  8.12 us (7%)
    pallas_call x1, Pallas kernels, body(): pl.pallas_call(functools.partial(kernel, shards, groups), out_shape=jax.S...  103 us
    unnamed x1, local copies, waits for them, and re-layouts  8.12 us

profile of v1, /device:TPU:0, one launch (start us, length us, event | category | flops | bytes accessed | tf_op | source)
XLA Modules:
  0.0 111.2 jit_solution(15267413022238160183)
XLA Ops:
  0.0 103.0 %shard_map.28 = f32[16,1,256,512]{3,2,1,0:T(8,128)} custom-call(f32[512,1024]{1,0:T(8,128)} %geno_ref.1, s32[512,1024]{1,0:T(8,128)} %obs_ref.1), custom_call_target="tpu_custom_call" | custom-call | tf_op jit(solution)/shard_map/pallas_call | solution.py:291
  103.0 8.1 %copy.4 = f32[16,1,256,512]{3,2,1,0:T(8,128)} copy(f32[16,1,256,512]{3,2,1,0:T(8,128)} %shard_map.28) | data formatting | bytes 16777216

commit v2 on v1

v2 whole, which is shorter than its diff:
```python
import functools

import jax
import jax.numpy as jnp
from jax import lax
from jax.experimental import pallas as pl
from jax.experimental.pallas import tpu as pltpu
from jax.sharding import PartitionSpec as P

MESH = pl.DeviceIdType.MESH
var_floor = 0.1
UP, DOWN, SIDE, CORE = 0, 1, 2, 3
STRIP = 64
PIECES = 2
LOADS = 4
VMEM_ALL = 67043328
VMEM_SPARE = 512 * 1024
VMEM_FINISH = 12 * 1024 * 1024


def index(at_z, at_y, at_core):
    return at_z * 4 + at_y * 2 + at_core


def source_at(z, depth, i):
    pairs = jnp.minimum(z, depth - 1 - z)
    side = jnp.where(i % 2 == 1, z - (i + 1) // 2, z + i // 2)
    far = jnp.where(z < depth - 1 - z, z + i - pairs, z - i + pairs)
    return jnp.where(i <= 2 * pairs, side, far)


def turned_at(z, depth):
    return jnp.where(z < depth - 1, z + 1, depth - 2)


def product(rows, panel, q):
    groups, pieces, piece_rows, snp_count = rows.shape[1:]
    total = None
    for h in range(groups):
        block = rows[q, h].reshape(pieces * piece_rows, snp_count)
        term = lax.dot_general(block, panel[h], (((1,), (1,)), ((), ())), preferred_element_type=jnp.float32)
        total = term if total is None else total + term
    return total * (1.0 / (groups * snp_count))


def finish(shards, groups, rows, panel, tiles, out_ref, late, out_sem):
    depth = shards // 4
    me = lax.axis_index("samp")
    z, y = me // 4, (me // 2) % 2
    turned = turned_at(z, depth)
    final = source_at(z, depth, depth - 1)
    final = jnp.where(final == turned, source_at(z, depth, depth - 2), final)

    def is_late(q):
        return ((q // 4 == turned) | (q // 4 == final)) & ((q // 2) % 2 != y)

    def put(q, carry):
        @pl.when(jnp.logical_not(is_late(q)))
        def _():
            pltpu.make_async_copy(tiles.at[q], out_ref.at[q, 0], out_sem.at[q]).start()

        return carry

    lax.fori_loop(0, shards, put, 0)

    def form(i, carry):
        q = index(jnp.where(i // 2 == 0, final, turned), 1 - y, lax.rem(i, 2))
        late[i] = product(rows, panel, q)
        pltpu.make_async_copy(late.at[i], out_ref.at[q, 0], out_sem.at[q]).start()
        return carry

    lax.fori_loop(0, 4, form, 0)

    def flush(q, carry):
        pltpu.make_async_copy(tiles.at[q], out_ref.at[q, 0], out_sem.at[q]).wait()
        return carry

    lax.fori_loop(0, shards, flush, 0)


def kernel(shards, groups, geno_hbm, obs_hbm, panel, rows, tiles, geno_ref, obs_ref, counts, load_sem,
           count_send, count_recv, panel_send, panel_recv, row_send, row_recv):
    row_count, snp_count = geno_ref.shape
    tile_rows = row_count // groups
    piece_rows = tile_rows // PIECES
    depth = shards // 4
    me = lax.axis_index("samp")
    part = lax.axis_index("snp")
    z, y, core = me // 4, (me // 2) % 2, me % 2

    load_rows = row_count // LOADS

    def load(i):
        block = pl.ds(pl.multiple_of(i * load_rows, load_rows), load_rows)
        return (pltpu.make_async_copy(geno_hbm.at[block], geno_ref.at[block], load_sem.at[0, i]),
                pltpu.make_async_copy(obs_hbm.at[block], obs_ref.at[block], load_sem.at[1, i]))

    for i in range(LOADS):
        for copy in load(i):
            copy.start()

    barrier = pltpu.get_barrier_semaphore()
    for step in range(1, shards):
        pl.semaphore_signal(barrier, inc=1, device_id={"samp": lax.rem(me + step, shards)}, device_id_type=MESH)
    for step in range(1, groups):
        pl.semaphore_signal(barrier, inc=1, device_id={"snp": lax.rem(part + step, groups)}, device_id_type=MESH)

    def add_strip(i, total):
        alt, call = total
        strip = pl.ds(pl.multiple_of(i * STRIP, STRIP), STRIP)
        present = obs_ref[strip, :].astype(jnp.float32)
        held = present * geno_ref[strip, :]
        for r in range(0, STRIP, 8):
            alt = alt + held[r:r + 8]
            call = call + present[r:r + 8]
        return alt, call

    zero = jnp.zeros((8, snp_count), jnp.float32)
    alt, call = zero, zero
    strips = load_rows // STRIP
    for i in range(LOADS):
        for copy in load(i):
            copy.wait()
        alt, call = lax.fori_loop(i * strips, (i + 1) * strips, add_strip, (alt, call))
    counts[me, 0:1, :] = jnp.sum(alt, axis=0, keepdims=True)
    counts[me, 1:2, :] = jnp.sum(call, axis=0, keepdims=True)

    pl.semaphore_wait(barrier, shards + groups - 2)

    def count_copy(owner, to):
        return pltpu.make_async_remote_copy(
            src_ref=counts.at[owner], dst_ref=counts.at[owner], send_sem=count_send.at[to],
            recv_sem=count_recv.at[owner], device_id={"samp": to}, device_id_type=MESH)

    for step in range(1, shards):
        count_copy(me, lax.rem(me + step, shards)).start()
    for step in range(1, shards):
        other = lax.rem(me + step, shards)
        count_copy(other, other).wait_recv()
    sums = counts[0]
    for s in range(1, shards):
        sums = sums + counts[s]
    frequency = sums[0:1] / (2.0 * jnp.maximum(sums[1:2], 1.0))
    shift = 2.0 * frequency
    gain = lax.rsqrt(jnp.maximum(shift * (1.0 - frequency), var_floor))

    def piece_of(k, p):
        return pl.ds(pl.multiple_of(k * tile_rows + p * piece_rows, piece_rows), piece_rows)

    def panel_copy(h, k, to, p):
        block = panel.at[h, piece_of(k, p)]
        return pltpu.make_async_remote_copy(
            src_ref=block, dst_ref=block, send_sem=panel_send.at[to, k, p],
            recv_sem=panel_recv.at[h, k, p], device_id={"snp": to}, device_id_type=MESH)

    strip_rows = min(STRIP, piece_rows)

    def scale_piece(k, p):
        def scale_strip(i, carry):
            start = pl.multiple_of(k * tile_rows + p * piece_rows + i * strip_rows, strip_rows)
            strip = pl.ds(start, strip_rows)
            present = obs_ref[strip, :].astype(jnp.float32)
            panel[part, strip, :] = (present * (geno_ref[strip, :] - shift) * gain).astype(jnp.bfloat16)
            return carry

        lax.fori_loop(0, piece_rows // strip_rows, scale_strip, 0)

    def row_copy(q, h, p, way, src=None):
        to = (index(z + 1, y, core), index(z - 1, y, core), index(z, 1 - y, core), index(z, y, 1 - core))[way]
        return pltpu.make_async_remote_copy(
            src_ref=rows.at[q, h, p] if src is None else src, dst_ref=rows.at[q, h, p],
            send_sem=row_send.at[way, q, h, p], recv_sem=row_recv.at[q, h, p],
            device_id={"samp": to}, device_id_type=MESH)

    def arrive(q, h, p):
        row_copy(q, h, p, CORE).wait_recv()

    last_part = lax.rem(part + groups - 1, groups)
    turned = turned_at(z, depth)

    def part_at(i):
        return lax.rem(part + i, groups)

    def send_own(h, p):
        mine = panel.at[h, piece_of(part, p)]
        row_copy(me, h, p, SIDE, mine).start()

        @pl.when(z < depth - 1)
        def _():
            row_copy(me, h, p, UP, mine).start()

        @pl.when(z > 0)
        def _():
            row_copy(me, h, p, DOWN, mine).start()

        row_copy(me, h, p, CORE, mine).start()
        rows[me, h, p] = panel[h, piece_of(part, p), :]

    for p in range(PIECES):
        for step in range(1, groups):
            other = part_at(step)
            scale_piece(other, p)
            panel_copy(part, other, other, p).start()
        scale_piece(part, p)
        send_own(part, p)
    for step in range(1, groups):
        other = part_at(step)
        for k in range(1, groups):
            for p in range(PIECES):
                panel_copy(part, lax.rem(other + k, groups), other, p).start()
    for step in range(1, groups):
        h = part_at(step)
        for p in range(PIECES):
            panel_copy(h, part, h, p).wait_recv()
            send_own(h, p)

    def column_arrival(at_z, h, p, way):
        q = index(at_z, y, core)
        arrive(q, h, p)

        @pl.when(z < depth - 1 if way == UP else z > 0)
        def _():
            row_copy(q, h, p, way).start()

        @pl.when((at_z != turned) | (h != last_part))
        def _():
            row_copy(q, h, p, SIDE).start()

        row_copy(q, h, p, CORE).start()

    def column_arrivals(i):
        def per_piece(t, carry):
            h, p = part_at(t // PIECES), lax.rem(t, PIECES)

            @pl.when(z - i >= 0)
            def _():
                column_arrival(z - i, h, p, UP)

            @pl.when(z + i < depth)
            def _():
                column_arrival(z + i, h, p, DOWN)

            return carry

        lax.fori_loop(0, groups * PIECES, per_piece, 0)

    def arrive_all(q):
        def per_piece(t, carry):
            arrive(q, t // PIECES, lax.rem(t, PIECES))
            return carry

        lax.fori_loop(0, groups * PIECES, per_piece, 0)

    def products(at_z, at_y):
        def per_core(t, carry):
            q = index(at_z, at_y, lax.rem(core + t, 2))

            @pl.when(t == 1)
            def _():
                arrive_all(q)

            tiles[q] = product(rows, panel, q)
            return carry

        lax.fori_loop(0, 2, per_core, 0)

    def side_arrival(at_z, h, p):
        q = index(at_z, 1 - y, core)
        arrive(q, h, p)
        row_copy(q, h, p, CORE).start()

    final = source_at(z, depth, depth - 1)
    final = jnp.where(final == turned, source_at(z, depth, depth - 2), final)

    def round_of(i, carry):
        @pl.when(i < depth)
        def _():
            column_arrivals(i)

        @pl.when(i == 1)
        def _():
            for step in range(1, groups):
                h = part_at(step)
                for k in range(1, groups):
                    for p in range(PIECES):
                        panel_copy(h, part_at(k), h, p).wait_recv()

        @pl.when(i == depth - 1)
        def _():
            q = index(z, 1 - y, core)

            @pl.when(z > 0)
            def _():
                for p in range(PIECES):
                    row_copy(q, last_part, p, DOWN).start()

            @pl.when(z == depth - 2)
            def _():
                for p in range(PIECES):
                    row_copy(q, last_part, p, UP).start()

        at_z = source_at(z, depth, i - 1)
        products(at_z, y)

        def per_piece(t, c):
            @pl.when((at_z != turned) | (t // PIECES != groups - 1))
            def _():
                side_arrival(at_z, part_at(t // PIECES), lax.rem(t, PIECES))

            return c

        lax.fori_loop(0, groups * PIECES, per_piece, 0)

        @pl.when((at_z != turned) & (at_z != final))
        def _():
            products(at_z, 1 - y)

        return carry

    lax.fori_loop(1, depth + 1, round_of, 0)
    for p in range(PIECES):
        side_arrival(turned, last_part, p)
    arrive_all(index(final, 1 - y, 1 - core))
    arrive_all(index(turned, 1 - y, 1 - core))

    for step in range(1, shards):
        count_copy(me, lax.rem(me + step, shards)).wait_send()
    for step in range(1, groups):
        for k in range(groups):
            for p in range(PIECES):
                panel_copy(part, k, part_at(step), p).wait_send()

    def drain(i, carry):
        at_z, h, p = i // (groups * PIECES), lax.rem(i // PIECES, groups), lax.rem(i, PIECES)
        q = index(at_z, y, core)
        across = index(at_z, 1 - y, core)

        @pl.when((at_z <= z) & (z < depth - 1))
        def _():
            row_copy(q, h, p, UP).wait_send()

        @pl.when((at_z >= z) & (z > 0))
        def _():
            row_copy(q, h, p, DOWN).wait_send()

        @pl.when((at_z != turned) | (h != last_part))
        def _():
            row_copy(q, h, p, SIDE).wait_send()

        row_copy(q, h, p, CORE).wait_send()
        row_copy(across, h, p, CORE).wait_send()

        @pl.when((at_z == z) & (h == last_part) & (z > 0))
        def _():
            row_copy(across, h, p, DOWN).wait_send()

        @pl.when((at_z == z) & (h == last_part) & (z == depth - 2))
        def _():
            row_copy(across, h, p, UP).wait_send()

        return carry

    lax.fori_loop(0, depth * groups * PIECES, drain, 0)


def solution(mesh):
    shards, groups = mesh.shape["samp"], mesh.shape["snp"]

    def body(genotypes, observed):
        row_count, snp_count = genotypes.shape
        tile_rows = row_count // groups
        piece_rows = tile_rows // PIECES
        kept = 2 * (groups * row_count * snp_count) * (1 + shards // groups) + 4 * shards * tile_rows * row_count
        panel, rows, tiles = pl.pallas_call(
            functools.partial(kernel, shards, groups),
            out_shape=(
                pltpu.VMEM((groups, row_count, snp_count), jnp.bfloat16),
                pltpu.VMEM((shards, groups, PIECES, piece_rows, snp_count), jnp.bfloat16),
                pltpu.VMEM((shards, tile_rows, row_count), jnp.float32),
            ),
            in_specs=[pl.BlockSpec(memory_space=pltpu.HBM)] * 2,
            out_specs=[pl.BlockSpec(memory_space=pltpu.VMEM)] * 3,
            scratch_shapes=[
                pltpu.VMEM((row_count, snp_count), jnp.float32),
                pltpu.VMEM((row_count, snp_count), jnp.int32),
                pltpu.VMEM((shards, 2, snp_count), jnp.float32),
                pltpu.SemaphoreType.DMA((2, LOADS)),
                pltpu.SemaphoreType.DMA((shards,)),
                pltpu.SemaphoreType.DMA((shards,)),
                pltpu.SemaphoreType.DMA((groups, groups, PIECES)),
                pltpu.SemaphoreType.DMA((groups, groups, PIECES)),
                pltpu.SemaphoreType.DMA((4, shards, groups, PIECES)),
                pltpu.SemaphoreType.DMA((shards, groups, PIECES)),
            ],
            compiler_params=pltpu.CompilerParams(
                collective_id=0, has_side_effects=True, vmem_limit_bytes=VMEM_ALL - VMEM_SPARE - kept),
        )(genotypes, observed)
        return pl.pallas_call(
            functools.partial(finish, shards, groups),
            out_shape=jax.ShapeDtypeStruct((shards, 1, tile_rows, row_count), jnp.float32),
            in_specs=[pl.BlockSpec(memory_space=pltpu.VMEM)] * 3,
            out_specs=pl.BlockSpec(memory_space=pltpu.HBM),
            scratch_shapes=[
                pltpu.VMEM((4, tile_rows, row_count), jnp.float32),
                pltpu.SemaphoreType.DMA((shards,)),
            ],
            compiler_params=pltpu.CompilerParams(vmem_limit_bytes=VMEM_FINISH),
        )(rows, panel, tiles)

    return jax.shard_map(
        body,
        mesh=mesh,
        in_specs=(P("samp", "snp"), P("samp", "snp")),
        out_specs=P(None, "snp", None, "samp"),
        check_vma=False,
    )
```

time: 111 us -> 101 us (0.910)
  local copies, waits for them, and re-layouts: 8.12 us -> 0 us
  Pallas kernels: 103 us -> 101 us
    unnamed x1 -> x0, local copies, waits for them, and re-layouts: 8.12 us -> none
    pallas_call x1 -> x2, Pallas kernels: 103 us -> 101 us  [the longest x1 96.8 us: body(): pl.pallas_call(functools.partial(kernel, shards, groups), out_shape=(pltp...]
where the time goes in v2:
time: 101 us
  Pallas kernels  101 us (100%)
    pallas_call x1, Pallas kernels, body(): pl.pallas_call(functools.partial(kernel, shards, groups), out_shape=(pltp...  96.8 us
    pallas_call x1, Pallas kernels, body(): pl.pallas_call(functools.partial(finish, shards, groups), out_shape=jax.S...  4.21 us

profile of v2, /device:TPU:0, one launch (start us, length us, event | category | flops | bytes accessed | tf_op | source)
XLA Modules:
  0.0 101.0 jit_solution(9724934660665844585)
XLA Ops:
  0.0 96.8 %shard_map.28 = (bf16[2,512,1024]{2,1,0:T(8,128)(2,1)S(1)}, bf16[16,2,2,128,1024]{4,3,2,1,0:T(8,128)(2,1)S(1)}, f32[16,256,512]{2,1,0:T(8,128)S(1)}) custom-call(f32[512,1024]{1,0:T(8,128)} %geno_hbm.1, s32[512,1024]{1,0:T(8,128)} %obs_hbm.1), custom_call_target="tpu_custom_call" | custom-call | tf_op jit(solution)/shard_map/pallas_call | solution.py:374
  96.8 4.2 %shard_map.29 = f32[16,1,256,512]{3,2,1,0:T(8,128)} custom-call(bf16[16,2,2,128,1024]{4,3,2,1,0:T(8,128)(2,1)S(1)} %get-tuple-element.8.rows, bf16[2,512,1024]{2,1,0:T(8,128)(2,1)S(1)} %get-tuple-element.9.panel, f32[16,256,512]{2,1,0:T(8,128)S(1)} %get-tuple-element.10.tiles), custom_call_target="tpu_custom_call" | custom-call | tf_op jit(solution)/shard_map/pallas_call | solution.py:398

commit v3 on v2

--- a/solution.py
+++ b/solution.py
@@ -33,14 +33,14 @@
     return jnp.where(z < depth - 1, z + 1, depth - 2)
 
 
-def product(rows, panel, q):
-    groups, pieces, piece_rows, snp_count = rows.shape[1:]
+def product(rows, panel, q, parts):
+    pieces, piece_rows, snp_count = rows.shape[2:]
     total = None
-    for h in range(groups):
+    for h in parts:
         block = rows[q, h].reshape(pieces * piece_rows, snp_count)
         term = lax.dot_general(block, panel[h], (((1,), (1,)), ((), ())), preferred_element_type=jnp.float32)
         total = term if total is None else total + term
-    return total * (1.0 / (groups * snp_count))
+    return total * (1.0 / (rows.shape[1] * snp_count))
 
 
 def finish(shards, groups, rows, panel, tiles, out_ref, late, out_sem):
@@ -50,6 +50,7 @@
     turned = turned_at(z, depth)
     final = source_at(z, depth, depth - 1)
     final = jnp.where(final == turned, source_at(z, depth, depth - 2), final)
+    last_part = lax.rem(lax.axis_index("snp") + groups - 1, groups)
 
     def is_late(q):
         return ((q // 4 == turned) | (q // 4 == final)) & ((q // 2) % 2 != y)
@@ -65,7 +66,7 @@
 
     def form(i, carry):
         q = index(jnp.where(i // 2 == 0, final, turned), 1 - y, lax.rem(i, 2))
-        late[i] = product(rows, panel, q)
+        late[i] = tiles[q] + product(rows, panel, q, [last_part])
         pltpu.make_async_copy(late.at[i], out_ref.at[q, 0], out_sem.at[q]).start()
         return carry
 
@@ -259,7 +260,7 @@
             def _():
                 arrive_all(q)
 
-            tiles[q] = product(rows, panel, q)
+            tiles[q] = product(rows, panel, q, range(groups))
             return carry
 
         lax.fori_loop(0, 2, per_core, 0)
@@ -271,6 +272,21 @@
 
     final = source_at(z, depth, depth - 1)
     final = jnp.where(final == turned, source_at(z, depth, depth - 2), final)
+
+    def begin_late():
+        def per_tile(t, carry):
+            q = index(jnp.where(t % 2 == 0, turned, final), 1 - y, lax.rem(core + t // 2, 2))
+
+            @pl.when(t >= 2)
+            def _():
+                for step in range(groups - 1):
+                    for p in range(PIECES):
+                        arrive(q, part_at(step), p)
+
+            tiles[q] = product(rows, panel, q, [part_at(step) for step in range(groups - 1)])
+            return carry
+
+        lax.fori_loop(0, 4, per_tile, 0)
 
     def round_of(i, carry):
         @pl.when(i < depth)
@@ -303,6 +319,10 @@
         products(at_z, y)
 
         def per_piece(t, c):
+            @pl.when((i == depth) & (t == (groups - 1) * PIECES))
+            def _():
+                begin_late()
+
             @pl.when((at_z != turned) | (t // PIECES != groups - 1))
             def _():
                 side_arrival(at_z, part_at(t // PIECES), lax.rem(t, PIECES))
@@ -320,8 +340,9 @@
     lax.fori_loop(1, depth + 1, round_of, 0)
     for p in range(PIECES):
         side_arrival(turned, last_part, p)
-    arrive_all(index(final, 1 - y, 1 - core))
-    arrive_all(index(turned, 1 - y, 1 - core))
+    for p in range(PIECES):
+        arrive(index(final, 1 - y, 1 - core), last_part, p)
+        arrive(index(turned, 1 - y, 1 - core), last_part, p)
 
     for step in range(1, shards):
         count_copy(me, lax.rem(me + step, shards)).wait_send()

time: 101 us -> 101 us (level)
  no operation moved by 1% of the time
where the time goes in v3:
time: 101 us; the launch traced here: 100 us
  Pallas kernels  100 us (99%)
    pallas_call x1, Pallas kernels, body(): pl.pallas_call(functools.partial(kernel, shards, groups), out_shape=(pltp...  96.8 us
    pallas_call x1, Pallas kernels, body(): pl.pallas_call(functools.partial(finish, shards, groups), out_shape=jax.S...  3.47 us

profile of v3, /device:TPU:0, one launch (start us, length us, event | category | flops | bytes accessed | tf_op | source)
XLA Modules:
  0.0 100.3 jit_solution(7075382922398213844)
XLA Ops:
  0.0 96.8 %shard_map.28 = (bf16[2,512,1024]{2,1,0:T(8,128)(2,1)S(1)}, bf16[16,2,2,128,1024]{4,3,2,1,0:T(8,128)(2,1)S(1)}, f32[16,256,512]{2,1,0:T(8,128)S(1)}) custom-call(f32[512,1024]{1,0:T(8,128)} %geno_hbm.1, s32[512,1024]{1,0:T(8,128)} %obs_hbm.1), custom_call_target="tpu_custom_call" | custom-call | tf_op jit(solution)/shard_map/pallas_call | solution.py:395
  96.8 3.5 %shard_map.29 = f32[16,1,256,512]{3,2,1,0:T(8,128)} custom-call(bf16[16,2,2,128,1024]{4,3,2,1,0:T(8,128)(2,1)S(1)} %get-tuple-element.8.rows, bf16[2,512,1024]{2,1,0:T(8,128)(2,1)S(1)} %get-tuple-element.9.panel, f32[16,256,512]{2,1,0:T(8,128)S(1)} %get-tuple-element.10.tiles), custom_call_target="tpu_custom_call" | custom-call | tf_op jit(solution)/shard_map/pallas_call | solution.py:419
